TPU v7x, 256 devices: a whole 4x4x8 slice. The times are simulated.
256 devices in a mesh: lat: 32 (over y, x, core), lev: 8 (over z).
Axes of the slice: x: 4, y: 4, z: 8, core: 2. Of those that a mesh axis runs over, the one named last changes fastest.
Arguments:
- fields: float32 [12, 128, 256, 1024], P(None, 'lev', 'lat'), may hold values from -6 to 6
- legendre: bfloat16 [256, 256, 256], P('lat'), as said below
- owner_counts: int32 [32], replicated, may hold values from 1 to 16, 256 in all
Outputs:
- covariance: float32 [512, 128, 128], P('lat', 'lev')
Inputs may be any that keep to these rules, and one draw needn't show every extreme that they name: `owner_counts`: each owner holds 1 to 16 total wavenumbers, the counts sum to 256, and some owner holds exactly 16. legendre[lat, m, n] is zero where n < m.
All inputs are finite; a program needn't handle non-finite values.
Results may differ from a plain program's by a relative error of at most 0.0038.
Values may be sent and summed in bfloat16 or wider, within the bound.
A program may use at most 128 MiB of HBM per device.

v0:
```python
import math

import jax
import jax.numpy as jnp
from jax import lax
from jax.sharding import PartitionSpec as P


def in_blocks(x, dim, length):
    before, after = (x.shape[:dim], x.shape[dim + 1 :])
    return jnp.moveaxis(x.reshape(*before, length, -1, *after), dim, 0)


def summed_on_arrival(x, axis, dim):
    parts = in_blocks(x, dim, lax.axis_size(axis))
    arrived = lax.all_to_all(parts, axis, split_axis=0, concat_axis=0, tiled=True)
    return arrived.astype(jnp.float32).sum(axis=0)


def fourier_table(points, modes):
    places = jnp.arange(points, dtype=jnp.int32)
    orders = jnp.arange(modes, dtype=jnp.int32)
    phase = places[:, None] * orders[None, :] % points
    angle = phase.astype(jnp.float32) * (2.0 * math.pi / points)
    factor = points ** (-0.5)
    return jnp.stack([jnp.cos(angle) * factor, -jnp.sin(angle) * factor], axis=2)


def on_device(fields, legendre, owner_counts):
    members, lev_rows, lat_rows, points = fields.shape
    modes = legendre.shape[1]
    lev_count = lax.axis_size("lev")
    owners = owner_counts.shape[0]
    capacity = 2 * modes // owners
    dft_table = fourier_table(points, modes)
    spectra = jnp.einsum("belx,xmc->lmcbe", fields, dft_table, precision=lax.Precision.HIGHEST)
    spectra = spectra.reshape(lat_rows, modes, 2 * members * lev_rows).astype(jnp.bfloat16)
    collected_rows, transform_table_rows = (
        lax.all_to_all(spectra, "lat", split_axis=1, concat_axis=0, tiled=True),
        lax.all_to_all(legendre, "lat", split_axis=1, concat_axis=0, tiled=True),
    )
    wavenumber_rows = jnp.einsum(
        "dez,det->tez", collected_rows, transform_table_rows, preferred_element_type=jnp.float32
    )
    resident_modes = wavenumber_rows.shape[1]
    shaped = wavenumber_rows.reshape(modes, resident_modes, 2, members, lev_rows)
    anomaly = (shaped - jnp.mean(shaped, axis=3, keepdims=True)).astype(jnp.bfloat16)
    anomaly = anomaly.reshape(modes, resident_modes, 2 * members * lev_rows)
    starts = jnp.cumsum(owner_counts) - owner_counts
    offset = jnp.arange(capacity, dtype=jnp.int32)
    active_flag = offset[None, :] < owner_counts[:, None]
    slot_index = jnp.where(active_flag, starts[:, None] + offset[None, :], 0).reshape(-1)
    slotted = jnp.take(anomaly, slot_index, axis=0)
    slotted = jnp.where(active_flag.reshape(-1)[:, None, None], slotted, jnp.zeros_like(slotted))
    slotted = slotted[None]
    received = lax.all_to_all(
        lax.all_to_all(slotted, "lat", split_axis=1, concat_axis=2, tiled=True),
        "lev",
        split_axis=2,
        concat_axis=0,
        tiled=True,
    )
    mode_share = received.shape[2]
    blocks = received.reshape(lev_count, capacity, mode_share, 2 * members, lev_rows)
    partial_value = jnp.einsum(
        "esaql,fsaqk->selfk", blocks, blocks, preferred_element_type=jnp.float32
    )
    partial_value = partial_value.reshape(capacity, lev_count * lev_rows, lev_count * lev_rows)
    summed = summed_on_arrival(partial_value.astype(jnp.bfloat16), "lev", 1)
    owner = lax.axis_index("lat")
    wavenumber = starts[owner] + offset
    live_count = owner_counts[owner]
    divisor = ((members - 1) * (2 * wavenumber + 2)).astype(jnp.float32)
    scaled = summed / divisor[:, None, None]
    return jnp.where((offset < live_count)[:, None, None], scaled, jnp.zeros_like(scaled))


def solution(mesh):
    return jax.shard_map(
        on_device,
        mesh=mesh,
        in_specs=(P(None, "lev", "lat", None), P("lat", None, None), P()),
        out_specs=P("lat", "lev", None),
        check_vma=False,
    )
```

profile of v0, /device:TPU:1, one launch (start us, length us, event | category | flops | bytes accessed | tf_op | source)
XLA Modules:
  0.0 276.8 jit_solution(14894597749513370844)
XLA Ops:
  0.0 4.2 %negate_multiply_fusion = (f32[1024,256,1]{1,0,2:T(8,128)S(1)}, f32[1024,256,1]{1,0,2:T(8,128)S(1)}) fusion(), kind=kLoop, calls=%fused_computation.27 | loop fusion | flops 4456448 | bytes 2097152 | tf_op jit(solution)/shard_map/mul | solution.py:26
  4.2 15.6 %fusion.13 = bf16[8,256,2,12,16]{1,4,0,3,2:T(8,128)(2,1)S(1)} fusion(f32[12,16,8,1024]{3,2,1,0:T(8,128)} %param.3, f32[1024,256,1]{1,0,2:T(8,128)S(1)} %get-tuple-element.7, f32[1024,256,1]{1,0,2:T(8,128)S(1)} %get-tuple-element.8), kind=kOutput, calls=%fused_computation.20 | convolution fusion | flops 9664987136 | bytes 9961472 | tf_op jit(solution)/shard_map/belx,xmc->lmcbe/dot_general | solution.py:36
  19.8 0.2 copy.20
  20.0 0.0 copy-start.1
  20.0 2.1 copy.21
  22.1 0.0 copy-start.2
  22.1 8.7 %all-to-all-start = ((bf16[8,256,384]{2,0,1:T(8,128)(2,1)}), bf16[8,256,384]{2,0,1:T(8,128)(2,1)S(1)}, u32[]{:S(2)}, u32[]{:S(2)}) async-start(bf16[8,256,384]{2,0,1:T(8,128)(2,1)} %copy.21), calls=%async_computation | async-start | bytes 3145728 | tf_op jit(solution)/shard_map/all_to_all | solution.py:39
  30.8 0.0 copy-done.1
  30.8 1.5 copy.24
  32.3 20.6 %all-to-all-done = bf16[8,256,384]{2,0,1:T(8,128)(2,1)S(1)} async-done(((bf16[8,256,384]{2,0,1:T(8,128)(2,1)}), bf16[8,256,384]{2,0,1:T(8,128)(2,1)S(1)}, u32[]{:S(2)}, u32[]{:S(2)}) %all-to-all-start) | async-done | bytes 1572896 | tf_op jit(solution)/shard_map/all_to_all | solution.py:39
  53.0 5.5 %all-to-all-start.1 = ((bf16[8,256,256]{2,0,1:T(8,128)(2,1)}), bf16[8,256,256]{2,0,1:T(8,128)(2,1)S(1)}, u32[]{:S(2)}, u32[]{:S(2)}) async-start(bf16[8,256,256]{2,0,1:T(8,128)(2,1)} %copy.24), calls=%async_computation.1 | async-start | bytes 2097152 | tf_op jit(solution)/shard_map/all_to_all | solution.py:40
  58.5 0.0 copy-done.2
  58.5 0.1 copy.18
  58.6 0.1 reduce-window.9
  58.7 0.1 reduce
  58.8 0.1 iota_add_fusion
  58.9 0.1 select_n.90
  59.0 0.1 add.89
  59.0 0.1 iota_compare_fusion
  59.1 0.1 lt.78
  59.3 1.4 copy.23
  60.7 15.0 %all-to-all-done.1 = bf16[8,256,256]{2,0,1:T(8,128)(2,1)S(1)} async-done(((bf16[8,256,256]{2,0,1:T(8,128)(2,1)}), bf16[8,256,256]{2,0,1:T(8,128)(2,1)S(1)}, u32[]{:S(2)}, u32[]{:S(2)}) %all-to-all-start.1) | async-done | bytes 1048608 | tf_op jit(solution)/shard_map/all_to_all | solution.py:40
  75.7 0.0 copy-start
  75.7 1.0 copy-done
  76.6 2.4 fusion.11
  79.1 0.4 reduce_sum.18
  79.5 1.5 fusion.5
  81.0 2.2 copy.27
  83.2 3.2 %gather_fusion = bf16[512,8,384]{2,1,0:T(8,128)(2,1)} fusion(bf16[256,8,384]{2,1,0:T(8,128)(2,1)S(1)} %copy.27, s32[1024]{0:T(1024)S(1)} %pad_clamp_fusion), kind=kCustom, calls=%fused_computation | custom fusion | bytes 6293504 | tf_op jit(solution)/shard_map/jit(_take)/gather | solution.py:53
  86.3 4.8 %fusion.4 = bf16[1,512,8,384]{3,2,0,1:T(8,128)(2,1)S(1)} fusion(bf16[512,8,384]{2,1,0:T(8,128)(2,1)} %gather_fusion, pred[512]{0:T(512)(128)(4,1)S(1)} %compare_and_fusion, pred[512]{0:T(512)(128)(4,1)S(1)} %lt.78), kind=kLoop, calls=%fused_computation.7 | loop fusion | flops 3145728 | bytes 6292480 | tf_op jit(solution)/shard_map/jit(_where)/select_n | solution.py:54
  91.1 43.1 %all_to_all.74 = bf16[1,512,8,384]{3,2,0,1:T(8,128)(2,1)S(1)} all-to-all(bf16[1,512,8,384]{3,2,0,1:T(8,128)(2,1)S(1)} %fusion.4), channel_id=1, replica_groups=mesh['lat'=32,'lev'=8] {'lat'}, dimensions={1} | all-to-all | bytes 6291456 | tf_op jit(solution)/shard_map/all_to_all | solution.py:57
  134.2 0.5 copy.55
  134.7 1.9 copy.30
  136.6 80.8 %all_to_all.75 = bf16[1,16,256,384]{3,1,0,2:T(8,128)(2,1)S(1)} all-to-all(bf16[1,16,256,384]{3,1,0,2:T(8,128)(2,1)S(1)} %copy.30), channel_id=1, replica_groups=mesh['lat'=32,'lev'=8] {'lev'}, dimensions={2} | all-to-all | bytes 6291456 | tf_op jit(solution)/shard_map/all_to_all | solution.py:56
  217.4 0.7 copy.31
  218.1 8.6 %copy.32 = bf16[8,1,16,32,384]{3,4,0,2,1:T(8,128)(2,1)} copy(bf16[8,1,16,32,384]{4,3,0,2,1:T(8,128)(2,1)S(1)} %bitcast.78) | data formatting | bytes 6291456 | tf_op jit(solution)/shard_map/all_to_all | solution.py:56
  226.7 19.8 %bitcast_convert_fusion = bf16[16,8,16,8,16]{4,2,3,1,0:T(8,128)(2,1)S(1)} fusion(bf16[8,16,32,24,16,1]{2,4,3,5,0,1:T(8,128)(2,1)} %bitcast.76, bf16[8,16,32,24,16,1]{2,4,3,0,5,1:T(8,128)(2,1)} %bitcast.77), kind=kOutput, calls=%fused_computation.1 | convolution fusion | flops 402915328 | bytes 6815744 | tf_op jit(solution)/shard_map/esaql,fsaqk->selfk/dot_general | solution.py:65
  246.6 4.0 %copy.33 = bf16[16,8,16,8,16]{4,3,2,1,0:T(8,128)(2,1)} copy(bf16[16,8,16,8,16]{4,2,3,1,0:T(8,128)(2,1)S(1)} %bitcast_convert_fusion) | data formatting | bytes 1048576 | tf_op jit(solution)/shard_map/convert_element_type | solution.py:69
  250.6 5.1 %convert_element_type.52 = bf16[16,8,16,128]{3,2,1,0:T(8,128)(2,1)S(1)} reshape(bf16[16,8,16,8,16]{4,3,2,1,0:T(8,128)(2,1)} %copy.33) | data formatting | bytes 1048576 | tf_op jit(solution)/shard_map/convert_element_type | solution.py:69
  255.7 0.8 copy.34
  256.5 3.5 %all-to-all-start.4 = ((bf16[8,16,16,128]{3,2,1,0:T(8,128)(2,1)}), bf16[8,16,16,128]{3,2,1,0:T(8,128)(2,1)S(1)}, u32[]{:S(2)}, u32[]{:S(2)}) async-start(bf16[8,16,16,128]{3,2,1,0:T(8,128)(2,1)} %copy.34), calls=%async_computation.4 | async-start | bytes 1048576 | tf_op jit(solution)/shard_map/all_to_all | solution.py:16
  260.0 0.6 dynamic_slice.7
  260.6 0.7 dynamic_slice.6
  261.3 0.7 multiply_convert_fusion
  262.0 0.7 iota_compare_fusion.1
  262.7 13.3 %all-to-all-done.4 = bf16[8,16,16,128]{3,2,1,0:T(8,128)(2,1)S(1)} async-done(((bf16[8,16,16,128]{3,2,1,0:T(8,128)(2,1)}), bf16[8,16,16,128]{3,2,1,0:T(8,128)(2,1)S(1)}, u32[]{:S(2)}, u32[]{:S(2)}) %all-to-all-start.4) | async-done | bytes 524320 | tf_op jit(solution)/shard_map/all_to_all | solution.py:16
  276.0 0.1 convert_reduce_fusion
  276.0 0.8 divide_select_fusion
  (5 shorter events, 0.1 us)
Async XLA Ops:
  20.0 10.8 %copy-start.1 = (bf16[8,256,256]{2,1,0:T(8,128)(2,1)S(1)}, bf16[8,256,256]{2,1,0:T(8,128)(2,1)}, u32[]{:S(2)}) copy-start(bf16[8,256,256]{2,1,0:T(8,128)(2,1)} %param.4) | copy-start | bytes 3145732
  22.1 36.5 %copy-start.2 = (s32[32]{0:T(128)S(1)}, s32[32]{0:T(128)}, u32[]{:S(2)}) copy-start(s32[32]{0:T(128)} %param.5) | copy-start | bytes 388
  22.1 30.9 %all-to-all-start = ((bf16[8,256,384]{2,0,1:T(8,128)(2,1)}), bf16[8,256,384]{2,0,1:T(8,128)(2,1)S(1)}, u32[]{:S(2)}, u32[]{:S(2)}) async-start(bf16[8,256,384]{2,0,1:T(8,128)(2,1)} %copy.21), calls=%async_computation | async-start | bytes 3145728 | tf_op jit(solution)/shard_map/all_to_all | solution.py:39
  53.0 22.7 %all-to-all-start.1 = ((bf16[8,256,256]{2,0,1:T(8,128)(2,1)}), bf16[8,256,256]{2,0,1:T(8,128)(2,1)S(1)}, u32[]{:S(2)}, u32[]{:S(2)}) async-start(bf16[8,256,256]{2,0,1:T(8,128)(2,1)} %copy.24), calls=%async_computation.1 | async-start | bytes 2097152 | tf_op jit(solution)/shard_map/all_to_all | solution.py:40
  75.7 1.0 copy-start
  256.5 19.4 %all-to-all-start.4 = ((bf16[8,16,16,128]{3,2,1,0:T(8,128)(2,1)}), bf16[8,16,16,128]{3,2,1,0:T(8,128)(2,1)S(1)}, u32[]{:S(2)}, u32[]{:S(2)}) async-start(bf16[8,16,16,128]{3,2,1,0:T(8,128)(2,1)} %copy.34), calls=%async_computation.4 | async-start | bytes 1048576 | tf_op jit(solution)/shard_map/all_to_all | solution.py:16
where the time goes:
time: 279 us; the launch traced here: 277 us
  blocking collectives  124 us (44%)
  waiting for transfers between devices  48.9 us (18%)
  matrix products  37.9 us (14%)
  local copies, waits for them, and re-layouts  34.8 us (12%)
  starting transfers between devices  17.7 us (6%)
  other arithmetic  13.4 us (5%)
    all_to_all x1, blocking collectives, on_device(): lax.all_to_all(lax.all_to_all(slotted, 'lat', split_axis=1, concat_axis=2...  80.8 us
    all_to_all x1, blocking collectives, on_device(): lax.all_to_all(slotted, 'lat', split_axis=1, concat_axis=2, tiled=True)  43.1 us
    all_to_all x1, waiting for transfers between devices, on_device(): lax.all_to_all(spectra, 'lat', split_axis=1, concat_axis=0, tiled=True)  20.6 us
    dot_general x1, matrix products, on_device(): jnp.einsum('esaql,fsaqk->selfk', blocks, blocks, preferred_element_type=j...  19.8 us
    dot_general x1, matrix products, on_device(): jnp.einsum('belx,xmc->lmcbe', fields, dft_table, precision=lax.Precision....  15.6 us
    all_to_all x1, waiting for transfers between devices, on_device(): lax.all_to_all(legendre, 'lat', split_axis=1, concat_axis=0, tiled=True)  15 us
    all_to_all x1, waiting for transfers between devices, summed_on_arrival(): lax.all_to_all(parts, axis, split_axis=0, concat_axis=0, tiled=True)  13.3 us
    all_to_all x2, local copies, waits for them, and re-layouts, on_device(): lax.all_to_all(lax.all_to_all(slotted, 'lat', split_axis=1, concat_axis=2...  9.36 us
  transfers between devices with their start and end apart: 3, of which 3 were waited for; matrix products, arithmetic and copies ran while one was open for 2% of the time, Pallas kernels for 0%

commit v1 on v0

v1 whole, which is shorter than its diff:
```python
import functools

import jax
import jax.numpy as jnp
import numpy as np
from jax import lax
from jax.experimental import pallas as pl
from jax.experimental.pallas import tpu as pltpu
from jax.sharding import PartitionSpec as P

MESH = pl.DeviceIdType.MESH
F32, BF16 = jnp.float32, jnp.bfloat16
PAIRS = ((0, 4), (1, 7), (2, 6), (3, 5))
UNITS = 5
UNIT_ORDER = (0, 4, 1, 2, 3)


def peer(me, k):
    chip, core = k // 2, k % 2
    dx = chip % 4
    dy = (chip // 4 + dx) % 4
    return ((me // 8 + dy) % 4) * 8 + ((me // 2 + dx) % 4) * 2 + (me + core) % 2


def kernel(
    spec, leg, counts, out,
    leg_out, leg_in, spec_in, packed, waves, anom_out, anom_in, mixed, swapped, part_out, part_in, cov, own_out, own_in,
    send_sem, recv_sem,
):
    me, zed = lax.axis_index("lat"), lax.axis_index("lev")
    lats, levs = 32, 8
    share = lats // levs
    sem_l, sem_s, sem_a, sem_z, sem_p, sem_o = 0, 1, 5, 10, 15, 16

    barrier = pltpu.get_barrier_semaphore()

    @pl.loop(1, lats)
    def _(k):
        pl.semaphore_signal(barrier, inc=1, device_id={"lat": peer(me, k)}, device_id_type=MESH)

    @pl.loop(1, levs)
    def _(k):
        pl.semaphore_signal(barrier, inc=1, device_id={"lev": (zed + k) % levs}, device_id_type=MESH)

    def over_lat(source, target, sem):
        @pl.loop(1, lats)
        def _(k):
            to = peer(me, k)
            pltpu.make_async_remote_copy(
                source.at[to], target.at[me], send_sem.at[sem], recv_sem.at[sem],
                device_id={"lat": to}, device_id_type=MESH,
            ).start()

        target[me] = source[me]

    def lat_copy(source, target, sem):
        return pltpu.make_async_remote_copy(
            source.at[pl.ds(0, lats - 1)], target.at[pl.ds(0, lats - 1)], send_sem.at[sem], recv_sem.at[sem],
            device_id={"lat": peer(me, 1)}, device_id_type=MESH,
        )

    column = lax.broadcasted_iota(jnp.int32, (32, 256), 1)
    for u in range(UNITS):
        for j in range(8):
            rows = leg[j, 32 * u : 32 * u + 32, :].astype(F32)
            if 0 < u < 4:
                other = leg[j, 32 * (8 - u) : 32 * (8 - u) + 32, :].astype(F32)
                rows = jnp.where(column < 32 * u, pltpu.roll(other, 32 * u, 1), rows)
            elif u == 4:
                rows = jnp.where(column < 128, 0.0, rows)
            for c in range(2):
                packed[c, pl.ds(j, 32, stride=8), :] = rows[:, 128 * c : 128 * c + 128]
        for c in range(2):
            leg_out[:, u, :, 128 * c : 128 * c + 128] = packed[c].astype(BF16).reshape(32, 8, 128)

    pl.semaphore_wait(barrier, lats - 1 + levs - 1)
    over_lat(leg_out, leg_in, sem_l)
    for g in range(4):
        over_lat(spec.at[g], spec_in.at[g], sem_s + g)
    lat_copy(leg_out, leg_in, sem_l).wait_recv()

    def transform(u, g, aa):
        return lax.dot_general(
            leg_in[:, u].reshape(256, 256), spec_in[g, :, aa].reshape(256, 384),
            (((0,), (0,)), ((), ())), preferred_element_type=F32,
        )

    def keep(value, low, high):
        for c in range(3):
            waves[c, low:high, :] = value[low:high, 128 * c : 128 * c + 128]

    def send_anomalies(u):
        @pl.loop(0, lats, unroll=4)
        def _(i):
            for c in range(3):
                anom_out[u, i, :, 128 * c : 128 * c + 128] = waves[c, pl.ds(i, 8, stride=32), :].astype(BF16)

        over_lat(anom_out.at[u], anom_in.at[u], sem_a + u)

    def lev_copy(u, to):
        return pltpu.make_async_remote_copy(
            anom_in.at[u, pl.ds(share * to, share)], mixed.at[u, zed], send_sem.at[sem_z + u], recv_sem.at[sem_z + u],
            device_id={"lev": to}, device_id_type=MESH,
        )

    def over_lev(u):
        lat_copy(anom_out.at[u], anom_in.at[u], sem_a + u).wait_recv()

        @pl.loop(1, levs)
        def _(k):
            lev_copy(u, (zed + k) % levs).start()

        mixed[u, zed] = anom_in[u, pl.ds(share * zed, share)]

    def lev_wait(u):
        return pltpu.make_async_remote_copy(
            mixed.at[u, pl.ds(0, levs - 1)], mixed.at[u, pl.ds(0, levs - 1)], send_sem.at[sem_z + u], recv_sem.at[sem_z + u],
            device_id={"lev": (zed + 1) % levs}, device_id_type=MESH,
        )

    for g in range(4):
        lat_copy(spec.at[g], spec_in.at[g], sem_s + g).wait_recv()
        if g == 0:
            keep(transform(0, 0, 0), 0, 256)
            send_anomalies(0)
            keep(transform(4, 0, 1), 0, 256)
            send_anomalies(4)
        else:
            keep(transform(g, g, 0), 32 * g, 256)
            keep(transform(g, g, 1), 0, 32 * g)
            send_anomalies(g)
        if g == 1:
            over_lev(0)
            over_lev(4)
        elif g > 1:
            over_lev(g - 1)
    over_lev(3)

    group = lax.broadcasted_iota(jnp.int32, (32, 128), 1) // 16
    for u in UNIT_ORDER:
        lev_wait(u).wait_recv()
        for j in range(3):
            v = [mixed[u, z, :, :, 128 * j : 128 * j + 128].astype(F32).reshape(32, 128) for z in range(8)]
            for bit in (1, 2, 4):
                high = (group // bit) % 2 == 1
                w = list(v)
                for i in range(8):
                    if i // bit % 2 == 0:
                        w[i] = jnp.where(high, pltpu.roll(v[i + bit], 16 * bit, 1), v[i])
                        w[i + bit] = jnp.where(high, v[i + bit], pltpu.roll(v[i], 128 - 16 * bit, 1))
                v = w
            for x in range(8):
                swapped[pl.ds(((u * 3 + j) * 8 + x) * 32, 32), :] = v[x]

    for b in range(8):
        rows = [(u, b) for u in range(min(b, 4) + 1)] + [(u, b - 8 + u) for u in range(max(1, 8 - b), 4)]
        x = jnp.concatenate([swapped[pl.ds(u * 768 + r, 96, stride=8), :] for u, r in rows], axis=0).astype(BF16)
        gram = lax.dot_general(x, x, (((0,), (0,)), ((), ())), preferred_element_type=F32)
        part_out[:, b] = gram.astype(BF16).reshape(8, 16, 128)

    @pl.loop(1, levs)
    def _(k):
        to = (zed + k) % levs
        pltpu.make_async_remote_copy(
            part_out.at[to], part_in.at[zed], send_sem.at[sem_p], recv_sem.at[sem_p],
            device_id={"lev": to}, device_id_type=MESH,
        ).start()

    part_in[zed] = part_out[zed]
    part_wait = pltpu.make_async_remote_copy(
        part_out.at[pl.ds(0, levs - 1)], part_in.at[pl.ds(0, levs - 1)], send_sem.at[sem_p], recv_sem.at[sem_p],
        device_id={"lev": (zed + 1) % levs}, device_id_type=MESH,
    )
    part_wait.wait_recv()
    for b in range(8):
        total = part_in[0, b].astype(F32)
        for z in range(1, 8):
            total += part_in[z, b].astype(F32)
        cov[b] = total / (11 * (2 * (32 * b + me) + 2)).astype(F32)

    def choose(d, start):
        n = start + (me + 512 - start) % 32
        own_out[d] = cov[jnp.minimum(n // 32, 7)]
        return start + counts[d]

    lax.fori_loop(0, lats, choose, jnp.int32(0))
    over_lat(own_out, own_in, sem_o)
    start = lax.fori_loop(0, lats, lambda d, t: t + jnp.where(d < me, counts[d], 0), jnp.int32(0))
    live = jnp.broadcast_to(counts[me], (16, 128))
    lat_copy(own_out, own_in, sem_o).wait_recv()
    for j in range(16):
        value = own_in[(start + j) % 32]
        out[j] = jnp.where(live > j, value, 0.0)

    lat_copy(leg_out, leg_in, sem_l).wait_send()
    for g in range(4):
        lat_copy(spec.at[g], spec_in.at[g], sem_s + g).wait_send()
    for u in range(UNITS):
        lat_copy(anom_out.at[u], anom_in.at[u], sem_a + u).wait_send()
        lev_wait(u).wait_send()
    part_wait.wait_send()
    lat_copy(own_out, own_in, sem_o).wait_send()


def fourier_tables():
    x = np.arange(512)
    a = np.array([a for pair in PAIRS for a in pair])
    tables = []
    for parity in range(2):
        m = 32 * a[:, None] + 2 * np.arange(16)[None, :] + parity
        angle = 2.0 * np.pi * ((x[:, None, None] * m[None]) % 1024) / 1024
        tables.append(np.stack([np.cos(angle), -np.sin(angle)], axis=-1) / 32.0)
    return np.stack(tables).astype(np.float32)


def on_device(fields, legendre, owner_counts):
    centred = fields - jnp.mean(fields, axis=0, keepdims=True)
    first, second = centred[..., :512], centred[..., 512:]
    tables = fourier_tables()
    halves = [
        jnp.einsum("belx,xakq->aklqbe", x, tables[p], precision=lax.Precision.HIGH)
        for p, x in enumerate((first + second, first - second))
    ]
    spec = jnp.stack(halves, axis=2).astype(BF16).reshape(4, 2, 32, 8, 384)
    spec = jnp.moveaxis(spec, 1, 2)
    vmem = pl.BlockSpec(memory_space=pltpu.VMEM)
    return pl.pallas_call(
        kernel,
        out_shape=jax.ShapeDtypeStruct((16, 16, 128), F32),
        in_specs=[vmem, vmem, pl.BlockSpec(memory_space=pltpu.SMEM)],
        out_specs=vmem,
        scratch_shapes=[
            pltpu.VMEM((32, UNITS, 8, 256), BF16),
            pltpu.VMEM((32, UNITS, 8, 256), BF16),
            pltpu.VMEM((4, 32, 2, 8, 384), BF16),
            pltpu.VMEM((2, 256, 128), F32),
            pltpu.VMEM((3, 256, 128), F32),
            pltpu.VMEM((UNITS, 32, 8, 384), BF16),
            pltpu.VMEM((UNITS, 32, 8, 384), BF16),
            pltpu.VMEM((UNITS, 8, 4, 8, 384), BF16),
            pltpu.VMEM((UNITS * 768, 128), F32),
            pltpu.VMEM((8, 8, 16, 128), BF16),
            pltpu.VMEM((8, 8, 16, 128), BF16),
            pltpu.VMEM((8, 16, 128), F32),
            pltpu.VMEM((32, 16, 128), F32),
            pltpu.VMEM((32, 16, 128), F32),
            pltpu.SemaphoreType.DMA((17,)),
            pltpu.SemaphoreType.DMA((17,)),
        ],
        compiler_params=pltpu.CompilerParams(
            collective_id=0, has_side_effects=True, vmem_limit_bytes=48 * 2**20
        ),
        name="exchange",
    )(spec, legendre, owner_counts)


def solution(mesh):
    return jax.shard_map(
        on_device,
        mesh=mesh,
        in_specs=(P(None, "lev", "lat", None), P("lat", None, None), P()),
        out_specs=P("lat", "lev", None),
        check_vma=False,
    )
```

time: 279 us -> 172 us (0.62)
  blocking collectives: 124 us -> 0 us
  Pallas kernels: 0 us -> 81.4 us
  waiting for transfers between devices: 48.9 us -> 0 us
  local copies, waits for them, and re-layouts: 34.8 us -> 55.5 us
  starting transfers between devices: 17.7 us -> 0 us
  matrix products: 37.9 us -> 20.7 us
    all_to_all x2 -> x0, blocking collectives: 124 us -> none  [the longest x1 80.8 us: on_device(): lax.all_to_all(lax.all_to_all(slotted, 'lat', split_axis=1, concat_axis=2...]
    pallas_call x0 -> x1, Pallas kernels: none -> 81.4 us  [on_device(): pl.pallas_call(kernel, out_shape=jax.ShapeDtypeStruct((16, 16, 128), F32)...]
    all_to_all x3 -> x0, waiting for transfers between devices: 48.9 us -> none  [the longest x1 20.6 us: on_device(): lax.all_to_all(spectra, 'lat', split_axis=1, concat_axis=0, tiled=True)]
    another operation x1, local copies, waits for them, and re-layouts: 0.09 us -> 36.1 us  [on_device(): spec = jnp.stack(halves, axis=2).astype(BF16).reshape(4, 2, 32, 8, 384)]
    all_to_all x3 -> x0, starting transfers between devices: 17.7 us -> none  [the longest x1 8.71 us: on_device(): lax.all_to_all(spectra, 'lat', split_axis=1, concat_axis=0, tiled=True)]
    dot_general x3 -> x2, matrix products: 37.9 us -> 20.7 us  [on_device(): jnp.einsum('belx,xakq->aklqbe', x, tables[p], precision=lax.Precision.HIGH)]
    all_to_all x5 -> x0, local copies, waits for them, and re-layouts: 13.1 us -> none  [the longest x2 9.36 us: on_device(): lax.all_to_all(lax.all_to_all(slotted, 'lat', split_axis=1, concat_axis=2...]
    another operation x2 -> x1, other arithmetic: 0.17 us -> 6.22 us  [on_device(): spec = jnp.stack(halves, axis=2).astype(BF16).reshape(4, 2, 32, 8, 384)]
  transfers between devices with their start and end apart: 3 -> 0, of which waited for: 3 -> 0; matrix products, arithmetic and copies ran while one was open for 2% -> 0% of each run, Pallas kernels for 0% -> 0%
where the time goes in v1:
time: 172 us; the launch traced here: 171 us
  Pallas kernels  81.4 us (47%)
  local copies, waits for them, and re-layouts  55.5 us (32%)
  matrix products  20.7 us (12%)
  other arithmetic  13.4 us (8%)
    pallas_call x1, Pallas kernels, on_device(): pl.pallas_call(kernel, out_shape=jax.ShapeDtypeStruct((16, 16, 128), F32)...  81.4 us
    another operation x1, local copies, waits for them, and re-layouts, on_device(): spec = jnp.stack(halves, axis=2).astype(BF16).reshape(4, 2, 32, 8, 384)  36.1 us
    dot_general x2, matrix products, on_device(): jnp.einsum('belx,xakq->aklqbe', x, tables[p], precision=lax.Precision.HIGH)  20.7 us
    convert_element_type x2, local copies, waits for them, and re-layouts, on_device(): spec = jnp.stack(halves, axis=2).astype(BF16).reshape(4, 2, 32, 8, 384)  18.7 us
    another operation x1, other arithmetic, on_device(): spec = jnp.stack(halves, axis=2).astype(BF16).reshape(4, 2, 32, 8, 384)  6.22 us
    sub x1, other arithmetic, on_device(): centred = fields - jnp.mean(fields, axis=0, keepdims=True)  3.71 us
    reduce_sum x1, other arithmetic, on_device(): centred = fields - jnp.mean(fields, axis=0, keepdims=True)  3.44 us

profile of v1, /device:TPU:1, one launch (start us, length us, event | category | flops | bytes accessed | tf_op | source)
XLA Modules:
  0.0 171.2 jit_solution(15800298245348256548)
XLA Ops:
  0.0 3.4 %reduce_sum.9 = f32[16,8,1024]{2,1,0:T(8,128)S(1)} reduce(f32[12,16,8,1024]{3,2,1,0:T(8,128)} %param.5, f32[]{:T(128)} %constant.3.clone.1), dimensions={0}, to_apply=%region_0.0 | reduce | flops 1441792 | bytes 6815748 | tf_op jit(solution)/shard_map/reduce_sum | solution.py:217
  3.5 0.0 copy-start.3
  3.5 3.7 %broadcast_subtract_fusion = f32[12,16,8,1024]{3,2,1,0:T(8,128)S(1)} fusion(f32[12,16,8,1024]{3,2,1,0:T(8,128)} %param.5, f32[16,8,1024]{2,1,0:T(8,128)S(1)} %broadcast_multiply_fusion), kind=kLoop, calls=%fused_computation.7 | loop fusion | flops 1572864 | bytes 13107200 | tf_op jit(solution)/shard_map/sub | solution.py:217
  7.2 0.0 copy-done.3
  7.2 0.0 copy-start.2
  7.3 10.4 %convert_bitcast_fusion.1 = bf16[8,16,1,8,2,12,16]{1,3,4,0,6,5,2:T(8,128)(2,1)S(1)} fusion(f32[512,8,16,2,1,1]{0,2,3,1,5,4:T(8,128)S(1)} %copy-done.3, f32[12,16,8,1024]{3,2,1,0:T(8,128)S(1)} %broadcast_subtract_fusion), kind=kOutput, calls=%fused_computation.2 | convolution fusion | flops 1209139200 | bytes 7602176 | tf_op jit(solution)/shard_map/belx,xakq->aklqbe/dot_general | solution.py:221
  17.6 0.0 copy-done.2
  17.7 10.4 %convert_bitcast_fusion = bf16[8,16,1,8,2,12,16]{1,3,4,0,6,5,2:T(8,128)(2,1)S(1)} fusion(f32[512,8,16,2,1,1]{0,2,3,1,5,4:T(8,128)S(1)} %copy-done.2, f32[12,16,8,1024]{3,2,1,0:T(8,128)S(1)} %broadcast_subtract_fusion), kind=kOutput, calls=%fused_computation.1 | convolution fusion | flops 1209139200 | bytes 7602176 | tf_op jit(solution)/shard_map/belx,xakq->aklqbe/dot_general | solution.py:221
  28.0 6.2 %pad_maximum_fusion = bf16[8,16,2,8,2,12,16]{1,3,4,0,6,5,2:T(8,128)(2,1)} fusion(bf16[8,16,1,8,2,12,16]{1,3,4,0,6,5,2:T(8,128)(2,1)S(1)} %convert_bitcast_fusion, bf16[8,16,1,8,2,12,16]{1,3,4,0,6,5,2:T(8,128)(2,1)S(1)} %convert_bitcast_fusion.1), kind=kLoop, calls=%fused_computation | loop fusion | flops 786432 | bytes 3145728 | tf_op jit(solution)/shard_map/stack | solution.py:224
  34.3 36.1 %copy.6 = bf16[8,16,2,8,2,12,16]{6,5,4,3,2,1,0:T(8,128)(2,1)} copy(bf16[8,16,2,8,2,12,16]{1,3,4,0,6,5,2:T(8,128)(2,1)} %pad_maximum_fusion) | data formatting | bytes 3145728 | tf_op jit(solution)/shard_map/stack | solution.py:224
  70.4 0.0 copy-start
  70.4 0.0 copy-start.1
  70.4 18.5 %convert_element_type.5 = bf16[4,2,32,8,384]{4,3,2,1,0:T(8,128)(2,1)S(1)} reshape(bf16[8,16,2,8,2,12,16]{6,5,4,3,2,1,0:T(8,128)(2,1)} %copy.6) | data formatting | bytes 3145728 | tf_op jit(solution)/shard_map/convert_element_type | solution.py:224
  88.9 0.2 copy.13
  89.1 0.0 copy-done
  89.1 0.0 copy-done.1
  89.1 81.4 %exchange.1 = f32[16,16,128]{2,1,0:T(8,128)S(1)} custom-call(bf16[4,32,2,8,384]{4,3,2,1,0:T(8,128)(2,1)S(1)} %bitcast.29, bf16[8,256,256]{2,1,0:T(8,128)(2,1)S(1)} %copy-done, s32[32]{0:T(128)S(1)} %copy-done.1), custom_call_target="tpu_custom_call" | custom-call | tf_op jit(solution)/shard_map/exchange/pallas_call | solution.py:227
  170.5 0.7 copy.15
  (1 shorter events, 0.0 us)
Async XLA Ops:
  3.5 3.7 %copy-start.3 = (f32[512,8,16,2,1,1]{0,2,3,1,5,4:T(8,128)S(1)}, f32[512,8,16,2,1,1]{0,2,3,1,5,4:T(8,128)}, u32[]{:S(2)}) copy-start(f32[512,8,16,2,1,1]{0,2,3,1,5,4:T(8,128)} %constant.13) | copy-start | bytes 1572868
  7.2 10.4 %copy-start.2 = (f32[512,8,16,2,1,1]{0,2,3,1,5,4:T(8,128)S(1)}, f32[512,8,16,2,1,1]{0,2,3,1,5,4:T(8,128)}, u32[]{:S(2)}) copy-start(f32[512,8,16,2,1,1]{0,2,3,1,5,4:T(8,128)} %constant.14) | copy-start | bytes 1572868
  70.4 18.7 %copy-start = (bf16[8,256,256]{2,1,0:T(8,128)(2,1)S(1)}, bf16[8,256,256]{2,1,0:T(8,128)(2,1)}, u32[]{:S(2)}) copy-start(bf16[8,256,256]{2,1,0:T(8,128)(2,1)} %leg.1) | copy-start | bytes 3145732
  70.4 18.7 %copy-start.1 = (s32[32]{0:T(128)S(1)}, s32[32]{0:T(128)}, u32[]{:S(2)}) copy-start(s32[32]{0:T(128)} %counts.1) | copy-start | bytes 388

commit v2 on v1

--- a/solution.py
+++ b/solution.py
@@ -22,16 +22,38 @@
     return ((me // 8 + dy) % 4) * 8 + ((me // 2 + dx) % 4) * 2 + (me + core) % 2
 
 
+def centred(v):
+    lane = lax.broadcasted_iota(jnp.int32, v[0].shape, 1)
+
+    def whole(t):
+        for shift in (64, 32, 16):
+            t = t + pltpu.roll(t, shift, 1)
+        return t
+
+    t = v[1]
+    for shift in (16, 32):
+        t = t + jnp.where((lane // shift) % 2 == 0, pltpu.roll(t, 128 - shift, 1), pltpu.roll(t, shift, 1))
+    other = pltpu.roll(t, 64, 1)
+    real = (whole(v[0]) + jnp.where(lane < 64, t, other)) * (1.0 / 12.0)
+    imag = (whole(v[2]) + jnp.where(lane < 64, other, t)) * (1.0 / 12.0)
+    return v[0] - real, v[1] - jnp.where(lane < 64, real, imag), v[2] - imag
+
+
 def kernel(
-    spec, leg, counts, out,
-    leg_out, leg_in, spec_in, packed, waves, anom_out, anom_in, mixed, swapped, part_out, part_in, cov, own_out, own_in,
-    send_sem, recv_sem,
+    fields, tables, leg, counts, out,
+    grid, table, spectra, spec, leg_out, leg_in, spec_in, packed, waves, anom_out, anom_in, mixed, swapped, part_out, part_in, cov, own_out, own_in,
+    send_sem, recv_sem, load_sem,
 ):
     me, zed = lax.axis_index("lat"), lax.axis_index("lev")
     lats, levs = 32, 8
     share = lats // levs
     sem_l, sem_s, sem_a, sem_z, sem_p, sem_o = 0, 1, 5, 10, 15, 16
 
+    loads = [pltpu.make_async_copy(tables, table, load_sem.at[8])] + [
+        pltpu.make_async_copy(fields.at[:, pl.ds(128 * c, 128)], grid.at[c], load_sem.at[c]) for c in range(8)
+    ]
+    for load in loads:
+        load.start()
     barrier = pltpu.get_barrier_semaphore()
 
     @pl.loop(1, lats)
@@ -42,16 +64,16 @@
     def _(k):
         pl.semaphore_signal(barrier, inc=1, device_id={"lev": (zed + k) % levs}, device_id_type=MESH)
 
-    def over_lat(source, target, sem):
+    def over_lat(source, target, sem, place=lambda to: to):
         @pl.loop(1, lats)
         def _(k):
             to = peer(me, k)
             pltpu.make_async_remote_copy(
-                source.at[to], target.at[me], send_sem.at[sem], recv_sem.at[sem],
+                source.at[place(to)], target.at[me], send_sem.at[sem], recv_sem.at[sem],
                 device_id={"lat": to}, device_id_type=MESH,
             ).start()
 
-        target[me] = source[me]
+        target[me] = source[place(me)]
 
     def lat_copy(source, target, sem):
         return pltpu.make_async_remote_copy(
@@ -75,8 +97,37 @@
 
     pl.semaphore_wait(barrier, lats - 1 + levs - 1)
     over_lat(leg_out, leg_in, sem_l)
+    for load in loads:
+        load.wait()
+
+    lane = lax.broadcasted_iota(jnp.int32, (128, 128), 1)
+
+    @pl.loop(0, 8)
+    def _(j):
+        for p in range(2):
+            high, low = [], []
+            for c in range(4):
+                first = grid[c, pl.ds(j, 192, stride=8), :]
+                second = grid[c + 4, pl.ds(j, 192, stride=8), :]
+                value = first + second if p == 0 else first - second
+                high.append(value.astype(BF16))
+                low.append((value - high[-1].astype(F32)).astype(BF16))
+            right = jnp.concatenate(high + low + high, axis=1)
+            right = jnp.concatenate([right, jnp.zeros((64, 1536), BF16)], axis=0)
+            left = jnp.concatenate([table[p, :, :512], table[p, :, :512], table[p, :, 512:]], axis=1)
+            sums = lax.dot_general(left, right, (((1,), (1,)), ((), ())), preferred_element_type=F32)
+            rows = pl.ds(1024 * p + j, 128, stride=8)
+            spectra[0, rows, :] = sums[:128, :128]
+            spectra[1, rows, :] = jnp.where(lane < 64, sums[:128, 128:], pltpu.roll(sums[128:, 128:], 64, 1))
+            spectra[2, rows, :] = sums[128:, :128]
+
     for g in range(4):
-        over_lat(spec.at[g], spec_in.at[g], sem_s + g)
+        for aa in range(2):
+            for p in range(2):
+                for c in range(3):
+                    value = spectra[c, pl.ds(1024 * p + 128 * (2 * g + aa), 128), :].astype(BF16)
+                    spec[g, 16 * p : 16 * p + 16, aa, :, 128 * c : 128 * c + 128] = value.reshape(16, 8, 128)
+        over_lat(spec.at[g], spec_in.at[g], sem_s + g, lambda to: 16 * (to % 2) + to // 2)
     lat_copy(leg_out, leg_in, sem_l).wait_recv()
 
     def transform(u, g, aa):
@@ -90,10 +141,14 @@
             waves[c, low:high, :] = value[low:high, 128 * c : 128 * c + 128]
 
     def send_anomalies(u):
-        @pl.loop(0, lats, unroll=4)
-        def _(i):
-            for c in range(3):
-                anom_out[u, i, :, 128 * c : 128 * c + 128] = waves[c, pl.ds(i, 8, stride=32), :].astype(BF16)
+        @pl.loop(0, 4)
+        def _(t):
+            v = [
+                jnp.concatenate([waves[c, pl.ds(8 * t + i, 8, stride=32), :] for i in range(8)], axis=0)
+                for c in range(3)
+            ]
+            for c, value in enumerate(centred(v)):
+                anom_out[u, pl.ds(8 * t, 8), :, 128 * c : 128 * c + 128] = value.astype(BF16).reshape(8, 8, 128)
 
         over_lat(anom_out.at[u], anom_in.at[u], sem_a + u)
 
@@ -207,29 +262,28 @@
     a = np.array([a for pair in PAIRS for a in pair])
     tables = []
     for parity in range(2):
-        m = 32 * a[:, None] + 2 * np.arange(16)[None, :] + parity
-        angle = 2.0 * np.pi * ((x[:, None, None] * m[None]) % 1024) / 1024
-        tables.append(np.stack([np.cos(angle), -np.sin(angle)], axis=-1) / 32.0)
-    return np.stack(tables).astype(np.float32)
+        m = (32 * a[:, None] + 2 * np.arange(16)[None, :] + parity).reshape(-1)
+        angle = 2.0 * np.pi * ((m[:, None] * x[None]) % 1024) / 1024
+        exact = np.concatenate([np.cos(angle), -np.sin(angle)]) / 32.0
+        high = exact.astype(jnp.bfloat16)
+        low = (exact - high.astype(np.float64)).astype(jnp.bfloat16)
+        tables.append(np.concatenate([high, low], axis=1))
+    return np.stack(tables)
 
 
 def on_device(fields, legendre, owner_counts):
-    centred = fields - jnp.mean(fields, axis=0, keepdims=True)
-    first, second = centred[..., :512], centred[..., 512:]
-    tables = fourier_tables()
-    halves = [
-        jnp.einsum("belx,xakq->aklqbe", x, tables[p], precision=lax.Precision.HIGH)
-        for p, x in enumerate((first + second, first - second))
-    ]
-    spec = jnp.stack(halves, axis=2).astype(BF16).reshape(4, 2, 32, 8, 384)
-    spec = jnp.moveaxis(spec, 1, 2)
     vmem = pl.BlockSpec(memory_space=pltpu.VMEM)
+    anywhere = pl.BlockSpec(memory_space=pl.ANY)
     return pl.pallas_call(
         kernel,
         out_shape=jax.ShapeDtypeStruct((16, 16, 128), F32),
-        in_specs=[vmem, vmem, pl.BlockSpec(memory_space=pltpu.SMEM)],
+        in_specs=[anywhere, anywhere, vmem, pl.BlockSpec(memory_space=pltpu.SMEM)],
         out_specs=vmem,
         scratch_shapes=[
+            pltpu.VMEM((8, 1536, 128), F32),
+            pltpu.VMEM((2, 256, 1024), BF16),
+            pltpu.VMEM((3, 2048, 128), F32),
+            pltpu.VMEM((4, 32, 2, 8, 384), BF16),
             pltpu.VMEM((32, UNITS, 8, 256), BF16),
             pltpu.VMEM((32, UNITS, 8, 256), BF16),
             pltpu.VMEM((4, 32, 2, 8, 384), BF16),
@@ -246,12 +300,13 @@
             pltpu.VMEM((32, 16, 128), F32),
             pltpu.SemaphoreType.DMA((17,)),
             pltpu.SemaphoreType.DMA((17,)),
+            pltpu.SemaphoreType.DMA((9,)),
         ],
         compiler_params=pltpu.CompilerParams(
             collective_id=0, has_side_effects=True, vmem_limit_bytes=48 * 2**20
         ),
         name="exchange",
-    )(spec, legendre, owner_counts)
+    )(fields.reshape(1536, 1024), jnp.asarray(fourier_tables()), legendre, owner_counts)
 
 
 def solution(mesh):

time: 172 us -> 87.2 us (0.51)
  local copies, waits for them, and re-layouts: 55.5 us -> 3.76 us
  matrix products: 20.7 us -> 0 us
  other arithmetic: 13.4 us -> 0 us
    another operation x1 -> x0, local copies, waits for them, and re-layouts: 36.1 us -> none  [on_device(): spec = jnp.stack(halves, axis=2).astype(BF16).reshape(4, 2, 32, 8, 384)]
    dot_general x2 -> x0, matrix products: 20.7 us -> none  [on_device(): jnp.einsum('belx,xakq->aklqbe', x, tables[p], precision=lax.Precision.HIGH)]
    convert_element_type x2 -> x0, local copies, waits for them, and re-layouts: 18.7 us -> none  [on_device(): spec = jnp.stack(halves, axis=2).astype(BF16).reshape(4, 2, 32, 8, 384)]
    another operation x1 -> x0, other arithmetic: 6.22 us -> none  [on_device(): spec = jnp.stack(halves, axis=2).astype(BF16).reshape(4, 2, 32, 8, 384)]
    sub x1 -> x0, other arithmetic: 3.71 us -> none  [on_device(): centred = fields - jnp.mean(fields, axis=0, keepdims=True)]
    reduce_sum x1 -> x0, other arithmetic: 3.44 us -> none  [on_device(): centred = fields - jnp.mean(fields, axis=0, keepdims=True)]
    unnamed x9 -> x7, local copies, waits for them, and re-layouts: 0.68 us -> 3.76 us
where the time goes in v2:
time: 87.2 us; the launch traced here: 86.8 us
  Pallas kernels  83 us (95%)
  local copies, waits for them, and re-layouts  3.76 us (4%)
    pallas_call x1, Pallas kernels, on_device(): pl.pallas_call(kernel, out_shape=jax.ShapeDtypeStruct((16, 16, 128), F32)...  83 us
    unnamed x7, local copies, waits for them, and re-layouts  3.76 us

profile of v2, /device:TPU:1, one launch (start us, length us, event | category | flops | bytes accessed | tf_op | source)
XLA Modules:
  0.0 86.8 jit_solution(1505622509769620987)
XLA Ops:
  0.0 0.0 copy-start
  0.0 1.2 %copy-done = bf16[8,256,256]{2,1,0:T(8,128)(2,1)S(1)} copy-done((bf16[8,256,256]{2,1,0:T(8,128)(2,1)S(1)}, bf16[8,256,256]{2,1,0:T(8,128)(2,1)}, u32[]{:S(2)}) %copy-start) | copy-done | bytes 1048600
  1.2 0.0 copy-start.1
  1.2 1.2 %copy-done.1 = bf16[2,256,1024]{2,1,0:T(8,128)(2,1)S(1)} copy-done((bf16[2,256,1024]{2,1,0:T(8,128)(2,1)S(1)}, bf16[2,256,1024]{2,1,0:T(8,128)(2,1)}, u32[]{:S(2)}) %copy-start.1) | copy-done | bytes 1048600
  2.5 0.0 copy-start.2
  2.5 0.7 copy-done.2
  3.1 83.0 %exchange.1 = f32[16,16,128]{2,1,0:T(8,128)S(1)} custom-call(f32[1536,1024]{1,0:T(8,128)} %bitcast.1, bf16[2,256,1024]{2,1,0:T(8,128)(2,1)S(1)} %copy-done.1, bf16[8,256,256]{2,1,0:T(8,128)(2,1)S(1)} %copy-done, s32[32]{0:T(128)S(1)} %copy-done.2), custom_call_target="tpu_custom_call" | custom-call | tf_op jit(solution)/shard_map/exchange/pallas_call | solution.py:277
  86.1 0.7 copy.6
Async XLA Ops:
  0.0 1.2 %copy-start = (bf16[8,256,256]{2,1,0:T(8,128)(2,1)S(1)}, bf16[8,256,256]{2,1,0:T(8,128)(2,1)}, u32[]{:S(2)}) copy-start(bf16[8,256,256]{2,1,0:T(8,128)(2,1)} %leg.1) | copy-start | bytes 3145732
  1.2 1.2 %copy-start.1 = (bf16[2,256,1024]{2,1,0:T(8,128)(2,1)S(1)}, bf16[2,256,1024]{2,1,0:T(8,128)(2,1)}, u32[]{:S(2)}) copy-start(bf16[2,256,1024]{2,1,0:T(8,128)(2,1)} %constant.2.clone.tables) | copy-start | bytes 3145732
  2.5 0.7 copy-start.2

commit v3 on v2

--- a/solution.py
+++ b/solution.py
@@ -15,13 +15,6 @@
 UNIT_ORDER = (0, 4, 1, 2, 3)
 
 
-def peer(me, k):
-    chip, core = k // 2, k % 2
-    dx = chip % 4
-    dy = (chip // 4 + dx) % 4
-    return ((me // 8 + dy) % 4) * 8 + ((me // 2 + dx) % 4) * 2 + (me + core) % 2
-
-
 def centred(v):
     lane = lax.broadcasted_iota(jnp.int32, v[0].shape, 1)
 
@@ -40,47 +33,50 @@
 
 
 def kernel(
-    fields, tables, leg, counts, out,
-    grid, table, spectra, spec, leg_out, leg_in, spec_in, packed, waves, anom_out, anom_in, mixed, swapped, part_out, part_in, cov, own_out, own_in,
+    fields, tables, leg_hbm, counts_hbm, out,
+    leg, counts, grid, table, spectra, spec, leg_out, leg_in, spec_in, packed, waves, anom_out, anom_in, mixed, swapped, total, part_out, part_in, cov, own_out, own_in,
     send_sem, recv_sem, load_sem,
 ):
     me, zed = lax.axis_index("lat"), lax.axis_index("lev")
     lats, levs = 32, 8
     share = lats // levs
-    sem_l, sem_s, sem_a, sem_z, sem_p, sem_o = 0, 1, 5, 10, 15, 16
-
-    loads = [pltpu.make_async_copy(tables, table, load_sem.at[8])] + [
+    sem_l, sem_s, sem_a, sem_z, sem_p, sem_o = 0, 1, 5, 10, 15, 17
+    sent, arriving = [], {}
+
+    load_leg = pltpu.make_async_copy(leg_hbm, leg, load_sem.at[9])
+    load_leg.start()
+    loads = [pltpu.make_async_copy(tables, table, load_sem.at[8]), pltpu.make_async_copy(counts_hbm, counts, load_sem.at[10])] + [
         pltpu.make_async_copy(fields.at[:, pl.ds(128 * c, 128)], grid.at[c], load_sem.at[c]) for c in range(8)
     ]
     for load in loads:
         load.start()
+    chips_y = [(me // 8 + d) % 4 for d in range(4)]
+    chips_x = [(me // 2 + d) % 4 for d in range(4)]
+    cores = [me % 2, 1 - me % 2]
+    chips = [4 * chips_y[(i // 4 + i) % 4] + chips_x[i % 4] for i in range(16)]
+    partners = [(2 * chips[k // 2] + cores[k % 2], chips[k // 2] + 16 * cores[k % 2]) for k in range(32)]
+    planes = [(zed + k) % levs for k in (1, 7, 2, 6, 3, 5, 4)]
+
     barrier = pltpu.get_barrier_semaphore()
-
-    @pl.loop(1, lats)
-    def _(k):
-        pl.semaphore_signal(barrier, inc=1, device_id={"lat": peer(me, k)}, device_id_type=MESH)
-
-    @pl.loop(1, levs)
-    def _(k):
-        pl.semaphore_signal(barrier, inc=1, device_id={"lev": (zed + k) % levs}, device_id_type=MESH)
-
-    def over_lat(source, target, sem, place=lambda to: to):
-        @pl.loop(1, lats)
-        def _(k):
-            to = peer(me, k)
+    for to, _ in partners[1:]:
+        pl.semaphore_signal(barrier, inc=1, device_id={"lat": to}, device_id_type=MESH)
+    for to in planes:
+        pl.semaphore_signal(barrier, inc=1, device_id={"lev": to}, device_id_type=MESH)
+
+    def over_lat(source, target, sem, halves=False):
+        for to, half in partners[1:]:
             pltpu.make_async_remote_copy(
-                source.at[place(to)], target.at[me], send_sem.at[sem], recv_sem.at[sem],
+                source.at[half if halves else to], target.at[me], send_sem.at[sem], recv_sem.at[sem],
                 device_id={"lat": to}, device_id_type=MESH,
             ).start()
-
-        target[me] = source[place(me)]
-
-    def lat_copy(source, target, sem):
-        return pltpu.make_async_remote_copy(
+        target[me] = source[partners[0][1] if halves else me]
+        arriving[sem] = pltpu.make_async_remote_copy(
             source.at[pl.ds(0, lats - 1)], target.at[pl.ds(0, lats - 1)], send_sem.at[sem], recv_sem.at[sem],
-            device_id={"lat": peer(me, 1)}, device_id_type=MESH,
+            device_id={"lat": partners[1][0]}, device_id_type=MESH,
         )
-
+        sent.append(arriving[sem])
+
+    load_leg.wait()
     column = lax.broadcasted_iota(jnp.int32, (32, 256), 1)
     for u in range(UNITS):
         for j in range(8):
@@ -121,14 +117,17 @@
             spectra[1, rows, :] = jnp.where(lane < 64, sums[:128, 128:], pltpu.roll(sums[128:, 128:], 64, 1))
             spectra[2, rows, :] = sums[128:, :128]
 
-    for g in range(4):
+    def send_spectra(g):
         for aa in range(2):
             for p in range(2):
                 for c in range(3):
                     value = spectra[c, pl.ds(1024 * p + 128 * (2 * g + aa), 128), :].astype(BF16)
                     spec[g, 16 * p : 16 * p + 16, aa, :, 128 * c : 128 * c + 128] = value.reshape(16, 8, 128)
-        over_lat(spec.at[g], spec_in.at[g], sem_s + g, lambda to: 16 * (to % 2) + to // 2)
-    lat_copy(leg_out, leg_in, sem_l).wait_recv()
+        over_lat(spec.at[g], spec_in.at[g], sem_s + g, halves=True)
+
+    send_spectra(0)
+    send_spectra(1)
+    arriving.pop(sem_l).wait_recv()
 
     def transform(u, g, aa):
         return lax.dot_general(
@@ -152,29 +151,25 @@
 
         over_lat(anom_out.at[u], anom_in.at[u], sem_a + u)
 
-    def lev_copy(u, to):
-        return pltpu.make_async_remote_copy(
-            anom_in.at[u, pl.ds(share * to, share)], mixed.at[u, zed], send_sem.at[sem_z + u], recv_sem.at[sem_z + u],
-            device_id={"lev": to}, device_id_type=MESH,
+    def over_lev(source, target, sem):
+        for to in planes:
+            pltpu.make_async_remote_copy(
+                source(to), target(zed), send_sem.at[sem], recv_sem.at[sem],
+                device_id={"lev": to}, device_id_type=MESH,
+            ).start()
+        target(zed)[...] = source(zed)[...]
+        arriving[sem] = pltpu.make_async_remote_copy(
+            target(pl.ds(0, levs - 1)), target(pl.ds(0, levs - 1)), send_sem.at[sem], recv_sem.at[sem],
+            device_id={"lev": planes[0]}, device_id_type=MESH,
         )
-
-    def over_lev(u):
-        lat_copy(anom_out.at[u], anom_in.at[u], sem_a + u).wait_recv()
-
-        @pl.loop(1, levs)
-        def _(k):
-            lev_copy(u, (zed + k) % levs).start()
-
-        mixed[u, zed] = anom_in[u, pl.ds(share * zed, share)]
-
-    def lev_wait(u):
-        return pltpu.make_async_remote_copy(
-            mixed.at[u, pl.ds(0, levs - 1)], mixed.at[u, pl.ds(0, levs - 1)], send_sem.at[sem_z + u], recv_sem.at[sem_z + u],
-            device_id={"lev": (zed + 1) % levs}, device_id_type=MESH,
-        )
+        sent.append(arriving[sem])
+
+    def mix(u):
+        arriving.pop(sem_a + u).wait_recv()
+        over_lev(lambda to: anom_in.at[u, pl.ds(share * to, share)], lambda z: mixed.at[u, z], sem_z + u)
 
     for g in range(4):
-        lat_copy(spec.at[g], spec_in.at[g], sem_s + g).wait_recv()
+        arriving.pop(sem_s + g).wait_recv()
         if g == 0:
             keep(transform(0, 0, 0), 0, 256)
             send_anomalies(0)
@@ -184,16 +179,19 @@
             keep(transform(g, g, 0), 32 * g, 256)
             keep(transform(g, g, 1), 0, 32 * g)
             send_anomalies(g)
+        if g < 2:
+            send_spectra(g + 2)
         if g == 1:
-            over_lev(0)
-            over_lev(4)
+            mix(0)
+            mix(4)
         elif g > 1:
-            over_lev(g - 1)
-    over_lev(3)
+            mix(g - 1)
+    mix(3)
 
     group = lax.broadcasted_iota(jnp.int32, (32, 128), 1) // 16
-    for u in UNIT_ORDER:
-        lev_wait(u).wait_recv()
+
+    def swap(u):
+        arriving.pop(sem_z + u).wait_recv()
         for j in range(3):
             v = [mixed[u, z, :, :, 128 * j : 128 * j + 128].astype(F32).reshape(32, 128) for z in range(8)]
             for bit in (1, 2, 4):
@@ -207,31 +205,39 @@
             for x in range(8):
                 swapped[pl.ds(((u * 3 + j) * 8 + x) * 32, 32), :] = v[x]
 
+    def gram(b, units):
+        rows = [(u, b) for u in range(min(b, 4) + 1)] + [(u, b - 8 + u) for u in range(max(1, 8 - b), 4)]
+        x = [swapped[pl.ds(u * 768 + r, 96, stride=8), :] for u, r in rows if u in units]
+        x = jnp.concatenate(x, axis=0).astype(BF16)
+        return lax.dot_general(x, x, (((0,), (0,)), ((), ())), preferred_element_type=F32)
+
+    def reduce(sem, low, high):
+        over_lev(
+            lambda to: part_out.at[pl.ds(low, high - low), to], lambda z: part_in.at[pl.ds(low, high - low), z], sem
+        )
+
+    for u in (0, 4, 1, 2):
+        swap(u)
     for b in range(8):
-        rows = [(u, b) for u in range(min(b, 4) + 1)] + [(u, b - 8 + u) for u in range(max(1, 8 - b), 4)]
-        x = jnp.concatenate([swapped[pl.ds(u * 768 + r, 96, stride=8), :] for u, r in rows], axis=0).astype(BF16)
-        gram = lax.dot_general(x, x, (((0,), (0,)), ((), ())), preferred_element_type=F32)
-        part_out[:, b] = gram.astype(BF16).reshape(8, 16, 128)
-
-    @pl.loop(1, levs)
-    def _(k):
-        to = (zed + k) % levs
-        pltpu.make_async_remote_copy(
-            part_out.at[to], part_in.at[zed], send_sem.at[sem_p], recv_sem.at[sem_p],
-            device_id={"lev": to}, device_id_type=MESH,
-        ).start()
-
-    part_in[zed] = part_out[zed]
-    part_wait = pltpu.make_async_remote_copy(
-        part_out.at[pl.ds(0, levs - 1)], part_in.at[pl.ds(0, levs - 1)], send_sem.at[sem_p], recv_sem.at[sem_p],
-        device_id={"lev": (zed + 1) % levs}, device_id_type=MESH,
-    )
-    part_wait.wait_recv()
+        value = gram(b, (0, 4, 1, 2))
+        if b < 3:
+            part_out[b] = value.astype(BF16).reshape(8, 16, 128)
+        else:
+            total[b] = value
+        if b == 2:
+            reduce(sem_p, 0, 3)
+    swap(3)
+    for b in range(3, 8):
+        part_out[b] = (total[b] + gram(b, (3,))).astype(BF16).reshape(8, 16, 128)
+    reduce(sem_p + 1, 3, 8)
+    arriving.pop(sem_p).wait_recv()
     for b in range(8):
-        total = part_in[0, b].astype(F32)
+        if b == 3:
+            arriving.pop(sem_p + 1).wait_recv()
+        value = part_in[b, 0].astype(F32)
         for z in range(1, 8):
-            total += part_in[z, b].astype(F32)
-        cov[b] = total / (11 * (2 * (32 * b + me) + 2)).astype(F32)
+            value += part_in[b, z].astype(F32)
+        cov[b] = value / (11 * (2 * (32 * b + me) + 2)).astype(F32)
 
     def choose(d, start):
         n = start + (me + 512 - start) % 32
@@ -242,19 +248,13 @@
     over_lat(own_out, own_in, sem_o)
     start = lax.fori_loop(0, lats, lambda d, t: t + jnp.where(d < me, counts[d], 0), jnp.int32(0))
     live = jnp.broadcast_to(counts[me], (16, 128))
-    lat_copy(own_out, own_in, sem_o).wait_recv()
+    arriving.pop(sem_o).wait_recv()
     for j in range(16):
         value = own_in[(start + j) % 32]
         out[j] = jnp.where(live > j, value, 0.0)
 
-    lat_copy(leg_out, leg_in, sem_l).wait_send()
-    for g in range(4):
-        lat_copy(spec.at[g], spec_in.at[g], sem_s + g).wait_send()
-    for u in range(UNITS):
-        lat_copy(anom_out.at[u], anom_in.at[u], sem_a + u).wait_send()
-        lev_wait(u).wait_send()
-    part_wait.wait_send()
-    lat_copy(own_out, own_in, sem_o).wait_send()
+    for copy in sent:
+        copy.wait_send()
 
 
 def fourier_tables():
@@ -277,9 +277,11 @@
     return pl.pallas_call(
         kernel,
         out_shape=jax.ShapeDtypeStruct((16, 16, 128), F32),
-        in_specs=[anywhere, anywhere, vmem, pl.BlockSpec(memory_space=pltpu.SMEM)],
+        in_specs=[anywhere] * 4,
         out_specs=vmem,
         scratch_shapes=[
+            pltpu.VMEM((8, 256, 256), BF16),
+            pltpu.SMEM((32,), jnp.int32),
             pltpu.VMEM((8, 1536, 128), F32),
             pltpu.VMEM((2, 256, 1024), BF16),
             pltpu.VMEM((3, 2048, 128), F32),
@@ -293,17 +295,18 @@
             pltpu.VMEM((UNITS, 32, 8, 384), BF16),
             pltpu.VMEM((UNITS, 8, 4, 8, 384), BF16),
             pltpu.VMEM((UNITS * 768, 128), F32),
+            pltpu.VMEM((8, 128, 128), F32),
             pltpu.VMEM((8, 8, 16, 128), BF16),
             pltpu.VMEM((8, 8, 16, 128), BF16),
             pltpu.VMEM((8, 16, 128), F32),
             pltpu.VMEM((32, 16, 128), F32),
             pltpu.VMEM((32, 16, 128), F32),
-            pltpu.SemaphoreType.DMA((17,)),
-            pltpu.SemaphoreType.DMA((17,)),
-            pltpu.SemaphoreType.DMA((9,)),
+            pltpu.SemaphoreType.DMA((18,)),
+            pltpu.SemaphoreType.DMA((18,)),
+            pltpu.SemaphoreType.DMA((11,)),
         ],
         compiler_params=pltpu.CompilerParams(
-            collective_id=0, has_side_effects=True, vmem_limit_bytes=48 * 2**20
+            collective_id=0, has_side_effects=True, vmem_limit_bytes=63 * 2**20
         ),
         name="exchange",
     )(fields.reshape(1536, 1024), jnp.asarray(fourier_tables()), legendre, owner_counts)

time: 87.2 us -> 77.7 us (0.89)
  Pallas kernels: 83 us -> 76.1 us
  local copies, waits for them, and re-layouts: 3.76 us -> 1.57 us
    pallas_call x1, Pallas kernels: 83 us -> 76.1 us  [on_device(): pl.pallas_call(kernel, out_shape=jax.ShapeDtypeStruct((16, 16, 128), F32)...]
    unnamed x7 -> x1, local copies, waits for them, and re-layouts: 3.76 us -> 1.57 us
where the time goes in v3:
time: 77.7 us
  Pallas kernels  76.1 us (98%)
  local copies, waits for them, and re-layouts  1.57 us (2%)
    pallas_call x1, Pallas kernels, on_device(): pl.pallas_call(kernel, out_shape=jax.ShapeDtypeStruct((16, 16, 128), F32)...  76.1 us
    unnamed x1, local copies, waits for them, and re-layouts  1.57 us

profile of v3, /device:TPU:1, one launch (start us, length us, event | category | flops | bytes accessed | tf_op | source)
XLA Modules:
  0.0 77.7 jit_solution(17161515005482855851)
XLA Ops:
  0.0 76.1 %exchange.1 = f32[16,16,128]{2,1,0:T(8,128)} custom-call(f32[1536,1024]{1,0:T(8,128)} %bitcast.1, bf16[2,256,1024]{2,1,0:T(8,128)(2,1)} %constant.2.clone.tables, bf16[8,256,256]{2,1,0:T(8,128)(2,1)} %leg_hbm.1, s32[32]{0:T(128)} %counts_hbm.1), custom_call_target="tpu_custom_call" | custom-call | tf_op jit(solution)/shard_map/exchange/pallas_call | solution.py:277
  76.1 1.6 %copy.6 = f32[16,16,128]{2,1,0:T(8,128)} copy(f32[16,16,128]{2,1,0:T(8,128)} %exchange.1) | data formatting | bytes 262144

commit v4 on v3

v4 whole, which is shorter than its diff:
```python
import functools

import jax
import jax.numpy as jnp
import numpy as np
from jax import lax
from jax.experimental import pallas as pl
from jax.experimental.pallas import tpu as pltpu
from jax.sharding import PartitionSpec as P

MESH = pl.DeviceIdType.MESH
F32, BF16 = jnp.float32, jnp.bfloat16
UNITS = ((0,), (1, 7), (2, 6), (3, 5), (4,))


def centred(v):
    lane = lax.broadcasted_iota(jnp.int32, v[0].shape, 1)

    def whole(t):
        for shift in (64, 32, 16):
            t = t + pltpu.roll(t, shift, 1)
        return t

    t = v[1]
    for shift in (16, 32):
        t = t + jnp.where((lane // shift) % 2 == 0, pltpu.roll(t, 128 - shift, 1), pltpu.roll(t, shift, 1))
    other = pltpu.roll(t, 64, 1)
    real = (whole(v[0]) + jnp.where(lane < 64, t, other)) * (1.0 / 12.0)
    imag = (whole(v[2]) + jnp.where(lane < 64, other, t)) * (1.0 / 12.0)
    return v[0] - real, v[1] - jnp.where(lane < 64, real, imag), v[2] - imag


def kernel(
    fields, tables, leg_hbm, counts_hbm, out,
    leg, counts, grid, table, spectra, spec_one, spec_two, leg_out, leg_half, leg_in, half_leg_in, into_one, into_two, packed, waves,
    anom_out, anom_half, anom_in, half_in, mixed, mixed_half, swapped, total, part_out, part_in, cov, own_out, own_in,
    send_sem, recv_sem, load_sem,
):
    me, zed = lax.axis_index("lat"), lax.axis_index("lev")
    lats, levs = 32, 8
    share = lats // levs
    sem_l, sem_s, sem_a, sem_z, sem_p, sem_o = 0, 3, 8, 13, 18, 20
    sent, arriving = [], {}
    spec = [(spec_one, (0,)), (spec_two, (0,)), (spec_two, (1,)), (spec_two, (2,)), (spec_one, (1,))]
    spec_in = [(into_one, (0,)), (into_two, (0,)), (into_two, (1,)), (into_two, (2,)), (into_one, (1,))]
    anomalies = [(anom_out, (u,)) for u in range(4)] + [(anom_half, ())]
    received = [(anom_in, (u,)) for u in range(4)] + [(half_in, ())]
    levels = [(mixed, (u,)) for u in range(4)] + [(mixed_half, ())]

    def view(part, index):
        ref, lead = part
        return ref.at[(*lead, index)]

    def read(part, *index):
        ref, lead = part
        return ref[(*lead, *index)]

    def store(part, value, *index):
        ref, lead = part
        ref[(*lead, *index)] = value

    every = slice(None)

    load_leg = pltpu.make_async_copy(leg_hbm, leg, load_sem.at[9])
    load_leg.start()
    loads = [pltpu.make_async_copy(tables, table, load_sem.at[8]), pltpu.make_async_copy(counts_hbm, counts, load_sem.at[10])] + [
        pltpu.make_async_copy(fields.at[:, pl.ds(128 * c, 128)], grid.at[c], load_sem.at[c]) for c in range(8)
    ]
    for load in loads:
        load.start()
    chips_y = [(me // 8 + d) % 4 for d in range(4)]
    chips_x = [(me // 2 + d) % 4 for d in range(4)]
    cores = [me % 2, 1 - me % 2]
    chips = [4 * chips_y[(i // 4 + i) % 4] + chips_x[i % 4] for i in range(16)]
    partners = [(2 * chips[k % 16] + cores[k // 16], chips[k % 16] + 16 * cores[k // 16]) for k in range(32)]
    planes = [(zed + k) % levs for k in (1, 7, 2, 6, 3, 5, 4)]

    barrier = pltpu.get_barrier_semaphore()
    for to, _ in partners[1:]:
        pl.semaphore_signal(barrier, inc=1, device_id={"lat": to}, device_id_type=MESH)
    for to in planes:
        pl.semaphore_signal(barrier, inc=1, device_id={"lev": to}, device_id_type=MESH)

    def over_lat(source, target, sem, halves=False):
        for to, half in partners[1:]:
            pltpu.make_async_remote_copy(
                view(source, half if halves else to), view(target, me), send_sem.at[sem], recv_sem.at[sem],
                device_id={"lat": to}, device_id_type=MESH,
            ).start()
        store(target, read(source, partners[0][1] if halves else me), me)
        arriving[sem] = pltpu.make_async_remote_copy(
            view(source, pl.ds(0, lats - 1)), view(target, pl.ds(0, lats - 1)), send_sem.at[sem], recv_sem.at[sem],
            device_id={"lat": partners[1][0]}, device_id_type=MESH,
        )
        sent.append(arriving[sem])

    load_leg.wait()
    column = lax.broadcasted_iota(jnp.int32, (32, 256), 1)
    for u in range(len(UNITS)):
        for j in range(8):
            rows = leg[j, 32 * u : 32 * u + 32, :].astype(F32)
            if 0 < u < 4:
                other = leg[j, 32 * (8 - u) : 32 * (8 - u) + 32, :].astype(F32)
                rows = jnp.where(column < 32 * u, pltpu.roll(other, 32 * u, 1), rows)
            for c in range(2):
                packed[c, pl.ds(j, 32, stride=8), :] = rows[:, 128 * c : 128 * c + 128]
        if u == 4:
            leg_half[...] = packed[1].astype(BF16).reshape(32, 8, 128)
        else:
            for c in range(2):
                leg_out[:, u, :, 128 * c : 128 * c + 128] = packed[c].astype(BF16).reshape(32, 8, 128)

    pl.semaphore_wait(barrier, lats - 1 + levs - 1)
    over_lat((leg_out, ()), (leg_in, ()), sem_l)
    for load in loads:
        load.wait()

    lane = lax.broadcasted_iota(jnp.int32, (128, 128), 1)

    @pl.loop(0, 8, unroll=2)
    def _(j):
        for p in range(2):
            high, low = [], []
            for c in range(4):
                first = grid[c, pl.ds(j, 192, stride=8), :]
                second = grid[c + 4, pl.ds(j, 192, stride=8), :]
                value = first + second if p == 0 else first - second
                high.append(value.astype(BF16))
                low.append((value - high[-1].astype(F32)).astype(BF16))
            right = jnp.concatenate(high + low + high, axis=1)
            right = jnp.concatenate([right, jnp.zeros((64, 1536), BF16)], axis=0)
            left = jnp.concatenate([table[p, :, :512], table[p, :, :512], table[p, :, 512:]], axis=1)
            sums = lax.dot_general(left, right, (((1,), (1,)), ((), ())), preferred_element_type=F32)
            rows = pl.ds(1024 * p + j, 128, stride=8)
            spectra[0, rows, :] = sums[:128, :128]
            spectra[1, rows, :] = jnp.where(lane < 64, sums[:128, 128:], pltpu.roll(sums[128:, 128:], 64, 1))
            spectra[2, rows, :] = sums[128:, :128]

    def send_spectra(u):
        first = sum(len(unit) for unit in UNITS[:u])
        for aa in range(len(UNITS[u])):
            for p in range(2):
                for c in range(3):
                    value = spectra[c, pl.ds(1024 * p + 128 * (first + aa), 128), :].astype(BF16)
                    value = value.reshape(16, 8, 128)
                    store(spec[u], value, pl.ds(16 * p, 16), aa, every, pl.ds(128 * c, 128))
        over_lat(spec[u], spec_in[u], sem_s + u, halves=True)

    send_spectra(0)
    send_spectra(1)
    over_lat((leg_half, ()), (half_leg_in, ()), sem_l + 2)
    arriving.pop(sem_l).wait_recv()

    def transform(u, aa):
        weights = half_leg_in[...].reshape(256, 128) if u == 4 else leg_in[:, u].reshape(256, 256)
        if aa == 1:
            weights = weights[:, :128]
        return lax.dot_general(
            weights, read(spec_in[u], every, aa).reshape(256, 384), (((0,), (0,)), ((), ())), preferred_element_type=F32
        )

    def keep(value, low, high):
        for c in range(3):
            waves[c, low:high, :] = value[low:high, 128 * c : 128 * c + 128]

    def send_anomalies(u):
        if u == 4:
            arriving.pop(sem_l + 2).wait_recv()
        arriving.pop(sem_s + u).wait_recv()
        if u < 4:
            keep(transform(u, 0), 32 * u, 256)
            if u > 0:
                keep(transform(u, 1), 0, 32 * u)
        else:
            value = transform(u, 0)
            v = centred([value[:, 128 * c : 128 * c + 128] for c in range(3)])
            waves[0, :128, :] = v[0]
            waves[0, 128:, :] = v[1]
            waves[1, :128, :] = v[2]

        @pl.loop(0, 4)
        def _(t):
            v = [
                jnp.concatenate([waves[c, pl.ds(8 * t + i, 8, stride=32), :] for i in range(8)], axis=0)
                for c in range(3 if u < 4 else 2)
            ]
            for c, value in enumerate(centred(v) if u < 4 else v):
                value = value.astype(BF16).reshape(8, 8, 128)
                store(anomalies[u], value, pl.ds(8 * t, 8), every, pl.ds(128 * c, 128))

        over_lat(anomalies[u], received[u], sem_a + u)

    def over_lev(source, target, sem):
        for to in planes:
            pltpu.make_async_remote_copy(
                source(to), target(zed), send_sem.at[sem], recv_sem.at[sem],
                device_id={"lev": to}, device_id_type=MESH,
            ).start()
        target(zed)[...] = source(zed)[...]
        arriving[sem] = pltpu.make_async_remote_copy(
            target(pl.ds(0, levs - 1)), target(pl.ds(0, levs - 1)), send_sem.at[sem], recv_sem.at[sem],
            device_id={"lev": planes[0]}, device_id_type=MESH,
        )
        sent.append(arriving[sem])

    def mix(u):
        arriving.pop(sem_a + u).wait_recv()
        over_lev(lambda to: view(received[u], pl.ds(share * to, share)), lambda z: view(levels[u], z), sem_z + u)

    group = lax.broadcasted_iota(jnp.int32, (32, 128), 1) // 16

    def swap(u):
        arriving.pop(sem_z + u).wait_recv()
        for j in range(3 if u < 4 else 2):
            v = [read(levels[u], z, every, every, pl.ds(128 * j, 128)).astype(F32).reshape(32, 128) for z in range(8)]
            for bit in (1, 2, 4):
                high = (group // bit) % 2 == 1
                w = list(v)
                for i in range(8):
                    if i // bit % 2 == 0:
                        w[i] = jnp.where(high, pltpu.roll(v[i + bit], 16 * bit, 1), v[i])
                        w[i + bit] = jnp.where(high, v[i + bit], pltpu.roll(v[i], 128 - 16 * bit, 1))
                v = w
            for x in range(8):
                swapped[pl.ds(((u * 3 + j) * 8 + x) * 32, 32), :] = v[x]

    send_anomalies(0)
    send_spectra(2)
    send_anomalies(1)
    send_spectra(3)
    mix(0)
    send_anomalies(2)
    send_spectra(4)
    mix(1)
    send_anomalies(3)
    mix(2)
    swap(0)
    send_anomalies(4)
    swap(1)
    mix(3)
    swap(2)
    mix(4)

    def gram(b, units):
        x = []
        for u in units:
            if u < 4:
                rows = [b] * (b >= u) + [b - 8 + u] * (8 - u <= b < 8)
                x += [swapped[pl.ds(768 * u + r, 96, stride=8), :] for r in rows if 0 <= r and (u > 0 or r == b)]
            elif b >= 4:
                x += [swapped[pl.ds(3072 + r, 32, stride=8), :] for r in (b - 4, b, 256 + b - 4)]
        x = jnp.concatenate(x, axis=0).astype(BF16)
        return lax.dot_general(x, x, (((0,), (0,)), ((), ())), preferred_element_type=F32)

    def reduce(sem, low, high):
        over_lev(
            lambda to: part_out.at[pl.ds(low, high - low), to], lambda z: part_in.at[pl.ds(low, high - low), z], sem
        )

    for b in range(8):
        total[b] = gram(b, (0, 1, 2))
    swap(3)
    for b in range(8):
        value = total[b] + gram(b, (3,)) if b >= 3 else total[b]
        if b < 4:
            part_out[b] = value.astype(BF16).reshape(8, 16, 128)
        else:
            total[b] = value
        if b == 3:
            reduce(sem_p, 0, 4)
    swap(4)
    for b in range(4, 8):
        part_out[b] = (total[b] + gram(b, (4,))).astype(BF16).reshape(8, 16, 128)
    reduce(sem_p + 1, 4, 8)
    arriving.pop(sem_p).wait_recv()
    for b in range(8):
        if b == 4:
            arriving.pop(sem_p + 1).wait_recv()
        value = part_in[b, 0].astype(F32)
        for z in range(1, 8):
            value += part_in[b, z].astype(F32)
        cov[b] = value / (11 * (2 * (32 * b + me) + 2)).astype(F32)

    def choose(d, start):
        n = start + (me + 512 - start) % 32
        own_out[d] = cov[jnp.minimum(n // 32, 7)]
        return start + counts[d]

    lax.fori_loop(0, lats, choose, jnp.int32(0))
    over_lat((own_out, ()), (own_in, ()), sem_o)
    start = lax.fori_loop(0, lats, lambda d, t: t + jnp.where(d < me, counts[d], 0), jnp.int32(0))
    live = jnp.broadcast_to(counts[me], (16, 128))
    arriving.pop(sem_o).wait_recv()
    for j in range(16):
        value = own_in[(start + j) % 32]
        out[j] = jnp.where(live > j, value, 0.0)

    for copy in sent:
        copy.wait_send()


def fourier_tables():
    x = np.arange(512)
    a = np.array([a for unit in UNITS for a in unit])
    tables = []
    for parity in range(2):
        m = (32 * a[:, None] + 2 * np.arange(16)[None, :] + parity).reshape(-1)
        angle = 2.0 * np.pi * ((m[:, None] * x[None]) % 1024) / 1024
        exact = np.concatenate([np.cos(angle), -np.sin(angle)]) / 32.0
        high = exact.astype(jnp.bfloat16)
        low = (exact - high.astype(np.float64)).astype(jnp.bfloat16)
        tables.append(np.concatenate([high, low], axis=1))
    return np.stack(tables)


def on_device(fields, legendre, owner_counts):
    vmem = pl.BlockSpec(memory_space=pltpu.VMEM)
    hbm = pl.BlockSpec(memory_space=pltpu.HBM)
    return pl.pallas_call(
        kernel,
        out_shape=jax.ShapeDtypeStruct((16, 16, 128), F32),
        in_specs=[hbm] * 4,
        out_specs=vmem,
        scratch_shapes=[
            pltpu.VMEM((8, 256, 256), BF16),
            pltpu.SMEM((32,), jnp.int32),
            pltpu.VMEM((8, 1536, 128), F32),
            pltpu.VMEM((2, 256, 1024), BF16),
            pltpu.VMEM((3, 2048, 128), F32),
            pltpu.VMEM((2, 32, 1, 8, 384), BF16),
            pltpu.VMEM((3, 32, 2, 8, 384), BF16),
            pltpu.VMEM((32, 4, 8, 256), BF16),
            pltpu.VMEM((32, 8, 128), BF16),
            pltpu.VMEM((32, 4, 8, 256), BF16),
            pltpu.VMEM((32, 8, 128), BF16),
            pltpu.VMEM((2, 32, 1, 8, 384), BF16),
            pltpu.VMEM((3, 32, 2, 8, 384), BF16),
            pltpu.VMEM((2, 256, 128), F32),
            pltpu.VMEM((3, 256, 128), F32),
            pltpu.VMEM((4, 32, 8, 384), BF16),
            pltpu.VMEM((32, 8, 256), BF16),
            pltpu.VMEM((4, 32, 8, 384), BF16),
            pltpu.VMEM((32, 8, 256), BF16),
            pltpu.VMEM((4, 8, 4, 8, 384), BF16),
            pltpu.VMEM((8, 4, 8, 256), BF16),
            pltpu.VMEM((3584, 128), F32),
            pltpu.VMEM((8, 128, 128), F32),
            pltpu.VMEM((8, 8, 16, 128), BF16),
            pltpu.VMEM((8, 8, 16, 128), BF16),
            pltpu.VMEM((8, 16, 128), F32),
            pltpu.VMEM((32, 16, 128), F32),
            pltpu.VMEM((32, 16, 128), F32),
            pltpu.SemaphoreType.DMA((21,)),
            pltpu.SemaphoreType.DMA((21,)),
            pltpu.SemaphoreType.DMA((11,)),
        ],
        compiler_params=pltpu.CompilerParams(
            collective_id=0, has_side_effects=True, vmem_limit_bytes=56_000_000
        ),
        name="exchange",
    )(fields.reshape(1536, 1024), jnp.asarray(fourier_tables()), legendre, owner_counts)


def solution(mesh):
    return jax.shard_map(
        on_device,
        mesh=mesh,
        in_specs=(P(None, "lev", "lat", None), P("lat", None, None), P()),
        out_specs=P("lat", "lev", None),
        check_vma=False,
    )
```

time: 77.7 us -> 73.4 us (0.945)
  Pallas kernels: 76.1 us -> 72 us
    pallas_call x1, Pallas kernels: 76.1 us -> 72 us  [on_device(): pl.pallas_call(kernel, out_shape=jax.ShapeDtypeStruct((16, 16, 128), F32)...]
    unnamed x1 -> x3, local copies, waits for them, and re-layouts: 1.57 us -> 1.31 us
where the time goes in v4:
time: 73.4 us; the launch traced here: 73.3 us
  Pallas kernels  72 us (98%)
  local copies, waits for them, and re-layouts  1.31 us (2%)
    pallas_call x1, Pallas kernels, on_device(): pl.pallas_call(kernel, out_shape=jax.ShapeDtypeStruct((16, 16, 128), F32)...  72 us

profile of v4, /device:TPU:1, one launch (start us, length us, event | category | flops | bytes accessed | tf_op | source)
XLA Modules:
  0.0 73.3 jit_solution(13303795939581693211)
XLA Ops:
  0.0 0.0 copy-start
  0.0 0.7 copy-done
  0.7 72.0 %exchange.1 = f32[16,16,128]{2,1,0:T(8,128)S(1)} custom-call(f32[1536,1024]{1,0:T(8,128)} %bitcast.1, bf16[2,256,1024]{2,1,0:T(8,128)(2,1)} %constant.2.clone.tables, bf16[8,256,256]{2,1,0:T(8,128)(2,1)} %leg_hbm.1, s32[32]{0:T(128)S(1)} %copy-done), custom_call_target="tpu_custom_call" | custom-call | tf_op jit(solution)/shard_map/exchange/pallas_call | solution.py:319
  72.7 0.7 copy.6
Async XLA Ops:
  0.0 0.7 copy-start
